TPU v7x, 512 devices: a whole 4x4x16 slice. The times are simulated.
512 devices in a mesh: tok: 8 (over x, core), vocab: 64 (over z, y).
Axes of the slice: x: 4, y: 4, z: 16, core: 2. Of those that a mesh axis runs over, the one named last changes fastest.
Arguments:
- hidden: bfloat16 [6144, 4096], P('tok', 'vocab'), as said below
- weight: bfloat16 [4096, 65536], P('tok', 'vocab'), may hold values from -0.09375 to 0.09375
- targets: int32 [6144], P('tok'), may hold values from 0 to 65535
- domains: int32 [6144], P('tok'), may hold values from 0 to 63
- seq_len: int32 [48], P('tok'), may hold values from 1 to 128
Outputs:
- token_loss: float32 [6144], P(('tok', 'vocab'))
- domain_mean: float32 [64], replicated
Inputs may be any that keep to these rules, and one draw needn't show every extreme that they name: hidden states of the eval window.
All inputs are finite; a program needn't handle non-finite values.
Results may differ from a plain program's by a relative error of at most 0.0003.
Values may be sent and summed in bfloat16 or wider, within the bound.
No kernel may reach another device: no remote copies, remote signals or barrier semaphores. Data moves between devices by JAX's collectives and lax.ppermute only.
A program may use at most 64 MiB of HBM per device.

v0:
```python
import jax
import jax.numpy as jnp
from jax import lax
from jax.sharding import Mesh
from jax.sharding import PartitionSpec as P

SEQ_LEN = 128
DOMAINS = 64
TOK = ("x", "c")
VOCAB = ("z", "y")
SWAP = [(0, 1), (1, 0)]


def to_all(array, axis, copies):
    return lax.all_to_all(
        jnp.broadcast_to(array[None], (copies, *array.shape)), axis, 0, 0, tiled=True
    )


def gathered_weight(weight):
    core = lax.axis_index("c")
    half = weight.shape[1] // 2
    keep = lax.dynamic_slice_in_dim(weight, core * half, half, 1)
    give = lax.dynamic_slice_in_dim(weight, (1 - core) * half, half, 1)
    other = lax.ppermute(give, "c", SWAP)
    rows = jnp.where(
        core == 0, jnp.concatenate([keep, other], 0), jnp.concatenate([other, keep], 0)
    )
    chips = lax.axis_size("x")
    own = to_all(rows, "x", chips).reshape(chips * rows.shape[0], half)
    return (own, lax.ppermute(own, "c", SWAP))


def tail(lse, picked, domains, seq_len):
    tokens = lse.shape[0]
    zs, ys = (lax.axis_size("z"), lax.axis_size("y"))
    own = tokens // (zs * ys)
    y = lax.axis_index("y")
    slices = jnp.stack([lse, picked]).reshape(2, zs, ys, own).transpose(2, 0, 1, 3)
    send = jnp.broadcast_to(slices.reshape(1, ys, -1), (zs, ys, 2 * zs * own))
    got = lax.all_to_all(send.reshape(zs * ys, -1), VOCAB, 0, 0, tiled=True)
    got = got.reshape(zs * ys, 2, zs * own)
    top = jnp.max(got[:, 0], axis=0)
    total = jnp.sum(jnp.exp(got[:, 0] - top[None]), axis=0)
    raw = jnp.log(total) + top - jnp.sum(got[:, 1], axis=0)
    index = lax.iota(jnp.int32, zs * own)
    local = index // own * (ys * own) + y * own + index % own
    seqs = seq_len.shape[0]
    lengths = jnp.sum(
        jnp.where(
            (local // SEQ_LEN)[:, None] == lax.broadcasted_iota(jnp.int32, (zs * own, seqs), 1),
            seq_len[None],
            0,
        ),
        axis=1,
    )
    mask = (local % SEQ_LEN < lengths).astype(jnp.float32)
    loss = raw * mask
    domain = lax.dynamic_index_in_dim(domains.reshape(zs, ys, own), y, 1, False).reshape(-1)
    here = domain[None, :] == lax.broadcasted_iota(jnp.int32, (DOMAINS, zs * own), 0)
    sums = jnp.sum(jnp.where(here, loss[None], 0.0), axis=1)
    counts = jnp.sum(jnp.where(here, mask[None], 0.0), axis=1)
    part = jnp.concatenate([sums, counts])
    axes = ("x", "c", "y")
    whole = jnp.sum(to_all(part, axes, lax.axis_size(axes)), axis=0)
    mean = whole[:DOMAINS] / jnp.maximum(whole[DOMAINS:], 1.0)
    token_loss = lax.dynamic_index_in_dim(loss.reshape(zs, own), lax.axis_index("z"), 0, False)
    return (token_loss, mean)


def body(hidden, weight, targets, domains, seq_len):
    features = lax.all_gather(hidden, "y", axis=1, tiled=True)
    features = lax.all_gather(features, "z", axis=1, tiled=True)
    core = lax.axis_index("c")
    halves = gathered_weight(weight)
    columns = weight.shape[1]
    half = columns // 2
    first = lax.axis_index(VOCAB) * columns
    logits = [jnp.dot(features, w, preferred_element_type=jnp.float32) for w in halves]
    tops = jnp.maximum(jnp.max(logits[0], axis=1), jnp.max(logits[1], axis=1))
    total, picked = (0.0, 0.0)
    for values, start in zip(logits, (core * half, (1 - core) * half)):
        ids = first + start + lax.broadcasted_iota(jnp.int32, values.shape, 1)
        total += jnp.sum(jnp.exp(values - tops[:, None]), axis=1)
        picked += jnp.sum(jnp.where(ids == targets[:, None], values, 0.0), axis=1)
    return tail(jnp.log(total) + tops, picked, domains, seq_len)


def solution(mesh):
    split = Mesh(mesh.devices.reshape(4, 2, 16, 4), ("x", "c", "z", "y"))
    placed = (P(TOK, VOCAB), P(TOK, VOCAB), P(TOK), P(TOK), P(TOK))
    return jax.shard_map(
        body, mesh=split, in_specs=placed, out_specs=(P((*TOK, *VOCAB)), P()), check_vma=False
    )
```

profile of v0, /device:TPU:1, one launch (start us, length us, event | category | flops | bytes accessed | tf_op | source)
XLA Modules:
  0.0 175.8 jit_solution(721808868574512698)
XLA Ops:
  7.2 13.0 %all_gather.6 = bf16[768,256]{0,1:T(8,128)(2,1)} all-gather(bf16[768,64]{0,1:T(8,128)(2,1)} %param.5), channel_id=1, replica_groups=mesh['x'=4,'c'=2,'z'=16,'y'=4] {'y'}, dimensions={1}, use_global_device_ids=true | all-gather | bytes 491520 | tf_op jit(solution)/shard_map/all_gather | solution.py:72
  20.2 1.3 constant_dynamic-slice_fusion.6
  21.5 9.2 %collective-permute-start = (bf16[512,512]{1,0:T(8,128)(2,1)S(1)}, bf16[512,512]{1,0:T(8,128)(2,1)S(1)}, u32[]{:S(2)}, u32[]{:S(2)}) collective-permute-start(bf16[512,512]{1,0:T(8,128)(2,1)S(1)} %get-tuple-element.17), channel_id=1, source_target_pairs={{0,64},{64,0},{1,65},{65,1},{2,66},{66,2},{3,67},{67,3},{4,68},{68... | collective-permute-start | bytes 1572872 | tf_op jit(solution)/shard_map/ppermute | solution.py:25
  30.7 1.5 collective-permute-done
  32.3 0.5 maximum_select_fusion
  32.7 0.3 broadcast_in_dim.65
  33.1 51.9 %all_to_all.20 = bf16[4,1024,512]{2,1,0:T(8,128)(2,1)} all-to-all(bf16[4,1024,512]{2,1,0:T(8,128)(2,1)S(1)} %broadcast_in_dim.65), channel_id=1, replica_groups=mesh['x'=4,'c'=2,'z'=16,'y'=4] {'x'}, dimensions={0} | all-to-all | bytes 8388608 | tf_op jit(solution)/shard_map/all_to_all | solution.py:15
  85.0 3.1 %collective-permute-start.1 = (bf16[4096,512]{1,0:T(8,128)(2,1)}, bf16[4096,512]{1,0:T(8,128)(2,1)}, u32[]{:S(2)}, u32[]{:S(2)}) collective-permute-start(bf16[4096,512]{1,0:T(8,128)(2,1)} %bitcast), channel_id=1, source_target_pairs={{0,64},{64,0},{1,65},{65,1},{2,66},{66,2},{3,67},{67,3},{4,68},{68... | collective-permute-start | bytes 12582920 | tf_op jit(solution)/shard_map/ppermute | solution.py:31
  88.3 20.7 %all-gather.2.cloned.1.call-done = bf16[768,4096]{0,1:T(8,128)(2,1)} async-done(((bf16[768,256]{0,1:T(8,128)(2,1)}), bf16[768,4096]{0,1:T(8,128)(2,1)}) %all-gather.2.cloned.1.call-update) | async-done | bytes 6291472 | tf_op jit(solution)/shard_map/all_gather | solution.py:73
  109.0 7.4 %fusion.28 = (f32[768]{0:T(1024)S(1)}, f32[512,768]{1,0:T(8,128)S(1)}) fusion(bf16[4096,512]{1,0:T(8,128)(2,1)} %bitcast, bf16[768,4096]{0,1:T(8,128)(2,1)} %all-gather.2.cloned.1.call-done), kind=kOutput, calls=%fused_computation.76 | convolution fusion | flops 3221617920 | bytes 12061696 | tf_op jit(solution)/shard_map/dot_general | solution.py:79
  116.5 5.3 %fusion.29 = (f32[768]{0:T(1024)S(1)}, f32[512,768]{1,0:T(8,128)S(1)}) fusion(bf16[4096,512]{1,0:T(8,128)(2,1)} %collective-permute-done.1, bf16[768,4096]{0,1:T(8,128)(2,1)S(1)} %copy-done.3), kind=kOutput, calls=%fused_computation.77 | convolution fusion | flops 3221617920 | bytes 12061696 | tf_op jit(solution)/shard_map/dot_general | solution.py:79
  121.8 0.8 fusion.4
  122.6 0.1 add.194
  123.0 0.7 all_to_all.14
  123.8 13.5 %all-to-all-start.1 = ((f32[64,1,384]{2,1,0:T(1,128)}), f32[64,1,384]{2,1,0:T(1,128)S(1)}, u32[]{:S(2)}, u32[]{:S(2)}) async-start(f32[64,1,384]{2,1,0:T(1,128)} %all_to_all.14), calls=%async_computation.1 | async-start | bytes 196608 | tf_op jit(solution)/shard_map/all_to_all | solution.py:41
  137.6 14.1 %all-to-all-done.1 = f32[64,1,384]{2,1,0:T(1,128)S(1)} async-done(((f32[64,1,384]{2,1,0:T(1,128)}), f32[64,1,384]{2,1,0:T(1,128)S(1)}, u32[]{:S(2)}, u32[]{:S(2)}) %all-to-all-start.1) | async-done | bytes 98336 | tf_op jit(solution)/shard_map/all_to_all | solution.py:41
  151.7 0.2 reduce.5
  152.0 0.1 reshape.233
  152.1 0.2 slice_reduce_fusion.1
  152.5 0.6 broadcast_in_dim.72
  153.1 8.3 %all-to-all-start.2 = ((f32[32,1,128]{2,1,0:T(1,128)}), f32[32,1,128]{2,1,0:T(1,128)S(1)}, u32[]{:S(2)}, u32[]{:S(2)}) async-start(f32[32,1,128]{2,1,0:T(1,128)} %broadcast_in_dim.72), calls=%async_computation.2 | async-start | bytes 32768 | tf_op jit(solution)/shard_map/all_to_all | solution.py:15
  161.5 0.5 fusion.25
  162.1 6.3 %all-to-all-done.2 = f32[32,1,128]{2,1,0:T(1,128)S(1)} async-done(((f32[32,1,128]{2,1,0:T(1,128)}), f32[32,1,128]{2,1,0:T(1,128)S(1)}, u32[]{:S(2)}, u32[]{:S(2)}) %all-to-all-start.2) | async-done | bytes 16416 | tf_op jit(solution)/shard_map/all_to_all | solution.py:15
  168.4 0.6 maximum_divide_fusion
  (35 shorter events, 1.2 us)
Async XLA Ops:
  7.2 101.9 %all-gather.2.cloned.1.call-start = ((), (), s32[]{:S(2)}) async-start(), calls=%async_computation.3 | async-start | bytes 6684672 | tf_op jit(solution)/shard_map/all_gather | solution.py:73
  21.5 10.7 %collective-permute-start = (bf16[512,512]{1,0:T(8,128)(2,1)S(1)}, bf16[512,512]{1,0:T(8,128)(2,1)S(1)}, u32[]{:S(2)}, u32[]{:S(2)}) collective-permute-start(bf16[512,512]{1,0:T(8,128)(2,1)S(1)} %get-tuple-element.17), channel_id=1, source_target_pairs={{0,64},{64,0},{1,65},{65,1},{2,66},{66,2},{3,67},{67,3},{4,68},{68... | collective-permute-start | bytes 1572872 | tf_op jit(solution)/shard_map/ppermute | solution.py:25
  33.1 55.1 %copy-start.2 = (s32[6]{0:T(128)S(1)}, s32[6]{0:T(128)}, u32[]{:S(2)}) copy-start(s32[6]{0:T(128)} %param.9) | copy-start | bytes 76
  85.0 31.5 %collective-permute-start.1 = (bf16[4096,512]{1,0:T(8,128)(2,1)}, bf16[4096,512]{1,0:T(8,128)(2,1)}, u32[]{:S(2)}, u32[]{:S(2)}) collective-permute-start(bf16[4096,512]{1,0:T(8,128)(2,1)} %bitcast), channel_id=1, source_target_pairs={{0,64},{64,0},{1,65},{65,1},{2,66},{66,2},{3,67},{67,3},{4,68},{68... | collective-permute-start | bytes 12582920 | tf_op jit(solution)/shard_map/ppermute | solution.py:31
  109.0 7.4 %copy-start.3 = (bf16[768,4096]{0,1:T(8,128)(2,1)S(1)}, bf16[768,4096]{0,1:T(8,128)(2,1)}, u32[]{:S(2)}) copy-start(bf16[768,4096]{0,1:T(8,128)(2,1)} %all-gather.2.cloned.1.call-done) | copy-start | bytes 18874372
  116.5 5.4 %copy-start = (s32[768]{0:T(1024)S(1)}, s32[768]{0:T(1024)}, u32[]{:S(2)}) copy-start(s32[768]{0:T(1024)} %param.7) | copy-start | bytes 9220
  121.8 15.5 %copy-start.1 = (s32[768]{0:T(1024)S(1)}, s32[768]{0:T(1024)}, u32[]{:S(2)}) copy-start(s32[768]{0:T(1024)} %param.8) | copy-start | bytes 9220
  123.8 28.0 %all-to-all-start.1 = ((f32[64,1,384]{2,1,0:T(1,128)}), f32[64,1,384]{2,1,0:T(1,128)S(1)}, u32[]{:S(2)}, u32[]{:S(2)}) async-start(f32[64,1,384]{2,1,0:T(1,128)} %all_to_all.14), calls=%async_computation.1 | async-start | bytes 196608 | tf_op jit(solution)/shard_map/all_to_all | solution.py:41
  153.1 15.2 %all-to-all-start.2 = ((f32[32,1,128]{2,1,0:T(1,128)}), f32[32,1,128]{2,1,0:T(1,128)S(1)}, u32[]{:S(2)}, u32[]{:S(2)}) async-start(f32[32,1,128]{2,1,0:T(1,128)} %broadcast_in_dim.72), calls=%async_computation.2 | async-start | bytes 32768 | tf_op jit(solution)/shard_map/all_to_all | solution.py:15
Sparse Core Ops, SparseCore 0:
  20.3 88.6 all-gather.1
where the time goes:
time: 176 us
  blocking collectives  64.9 us (37%)
  waiting for transfers between devices  42.7 us (24%)
  starting transfers between devices  34.1 us (19%)
  between operations  14.3 us (8%)
  matrix products  12.7 us (7%)
  local copies, waits for them, and re-layouts  3.85 us (2%)
  other arithmetic  3.23 us (2%)
    all_to_all x1, blocking collectives, to_all(): lax.all_to_all(jnp.broadcast_to(array[None], (copies, *array.shape)), axi...  51.9 us
    all_gather x1, waiting for transfers between devices, body(): features = lax.all_gather(features, 'z', axis=1, tiled=True)  20.7 us
    all_to_all x1, waiting for transfers between devices, tail(): got = lax.all_to_all(send.reshape(zs * ys, -1), VOCAB, 0, 0, tiled=True)  14.1 us
    all_to_all x1, starting transfers between devices, tail(): got = lax.all_to_all(send.reshape(zs * ys, -1), VOCAB, 0, 0, tiled=True)  13.5 us
    all_gather x1, blocking collectives, body(): features = lax.all_gather(hidden, 'y', axis=1, tiled=True)  13 us
    dot_general x2, matrix products, body(): jnp.dot(features, w, preferred_element_type=jnp.float32)  12.7 us
    ppermute x1, starting transfers between devices, gathered_weight(): other = lax.ppermute(give, 'c', SWAP)  9.23 us
    all_to_all x1, starting transfers between devices, to_all(): lax.all_to_all(jnp.broadcast_to(array[None], (copies, *array.shape)), axi...  8.29 us
  transfers between devices with their start and end apart: 5, of which 4 were waited for; matrix products, arithmetic and copies ran while one was open for 6% of the time, Pallas kernels for 0%

commit v1 on v0

--- a/solution.py
+++ b/solution.py
@@ -70,7 +70,10 @@
 
 def body(hidden, weight, targets, domains, seq_len):
     features = lax.all_gather(hidden, "y", axis=1, tiled=True)
-    features = lax.all_gather(features, "z", axis=1, tiled=True)
+    count = lax.axis_size("z")
+    shards = jnp.stack([features for _ in range(count)])
+    shards = lax.all_to_all(shards, "z", split_axis=0, concat_axis=0)
+    features = jnp.concatenate(shards, axis=1)
     core = lax.axis_index("c")
     halves = gathered_weight(weight)
     columns = weight.shape[1]

time: 176 us -> 415 us (2.36)
  waiting for transfers between devices: 42.7 us -> 328 us
  blocking collectives: 64.9 us -> 10.8 us
  starting transfers between devices: 34.1 us -> 47.8 us
  between operations: 14.3 us -> 0.9 us
  local copies, waits for them, and re-layouts: 3.85 us -> 9.05 us
    all_to_all x0 -> x1, waiting for transfers between devices: none -> 268 us  [body(): shards = lax.all_to_all(shards, 'z', split_axis=0, concat_axis=0)]
    all_to_all x1 -> x0, blocking collectives: 51.9 us -> none  [to_all(): lax.all_to_all(jnp.broadcast_to(array[None], (copies, *array.shape)), axi...]
    all_to_all x1 -> x2, waiting for transfers between devices: 6.33 us -> 44.2 us  [to_all(): lax.all_to_all(jnp.broadcast_to(array[None], (copies, *array.shape)), axi...]
    all_gather x1 -> x0, waiting for transfers between devices: 20.7 us -> none  [body(): features = lax.all_gather(features, 'z', axis=1, tiled=True)]
    all_to_all x0 -> x1, starting transfers between devices: none -> 9.75 us  [body(): shards = lax.all_to_all(shards, 'z', split_axis=0, concat_axis=0)]
    all_to_all x1 -> x2, starting transfers between devices: 8.29 us -> 11.3 us  [to_all(): lax.all_to_all(jnp.broadcast_to(array[None], (copies, *array.shape)), axi...]
  transfers between devices with their start and end apart: 5 -> 6, of which waited for: 4 -> 5; matrix products, arithmetic and copies ran while one was open for 6% -> 2% of each run, Pallas kernels for 0% -> 0%
where the time goes in v1:
time: 415 us; the launch traced here: 414 us
  waiting for transfers between devices  328 us (79%)
  starting transfers between devices  47.8 us (12%)
  matrix products  14.2 us (3%)
  blocking collectives  10.8 us (3%)
  local copies, waits for them, and re-layouts  9.05 us (2%)
    all_to_all x1, waiting for transfers between devices, body(): shards = lax.all_to_all(shards, 'z', split_axis=0, concat_axis=0)  268 us
    all_to_all x2, waiting for transfers between devices, to_all(): lax.all_to_all(jnp.broadcast_to(array[None], (copies, *array.shape)), axi...  44.2 us
    all_to_all x1, starting transfers between devices, tail(): got = lax.all_to_all(send.reshape(zs * ys, -1), VOCAB, 0, 0, tiled=True)  14.6 us
    all_to_all x1, waiting for transfers between devices, tail(): got = lax.all_to_all(send.reshape(zs * ys, -1), VOCAB, 0, 0, tiled=True)  14.3 us
    dot_general x2, matrix products, body(): jnp.dot(features, w, preferred_element_type=jnp.float32)  14.2 us
    all_to_all x2, starting transfers between devices, to_all(): lax.all_to_all(jnp.broadcast_to(array[None], (copies, *array.shape)), axi...  11.3 us
    all_gather x1, blocking collectives, body(): features = lax.all_gather(hidden, 'y', axis=1, tiled=True)  10.8 us
    all_to_all x1, starting transfers between devices, body(): shards = lax.all_to_all(shards, 'z', split_axis=0, concat_axis=0)  9.75 us
  transfers between devices with their start and end apart: 6, of which 5 were waited for; matrix products, arithmetic and copies ran while one was open for 2% of the time, Pallas kernels for 0%

profile of v1, /device:TPU:1, one launch (start us, length us, event | category | flops | bytes accessed | tf_op | source)
XLA Modules:
  0.0 414.2 jit_solution(9382721074768436457)
XLA Ops:
  0.6 1.3 constant_dynamic-slice_fusion.6
  1.9 8.7 %collective-permute-start = (bf16[512,512]{1,0:T(8,128)(2,1)S(1)}, bf16[512,512]{1,0:T(8,128)(2,1)S(1)}, u32[]{:S(2)}, u32[]{:S(2)}) collective-permute-start(bf16[512,512]{1,0:T(8,128)(2,1)S(1)} %get-tuple-element.17), channel_id=1, source_target_pairs={{0,64},{64,0},{1,65},{65,1},{2,66},{66,2},{3,67},{67,3},{4,68},{68... | collective-permute-start | bytes 1572872 | tf_op jit(solution)/shard_map/ppermute | solution.py:25
  10.7 1.5 collective-permute-done
  12.2 0.5 maximum_select_fusion
  12.6 2.2 broadcast_in_dim.65
  14.9 5.1 %all-to-all-start = ((bf16[4,1024,512]{2,1,0:T(8,128)(2,1)}), bf16[4,1024,512]{2,1,0:T(8,128)(2,1)}, u32[]{:S(2)}, u32[]{:S(2)}) async-start(bf16[4,1024,512]{2,1,0:T(8,128)(2,1)} %broadcast_in_dim.65), calls=%async_computation | async-start | bytes 8388608 | tf_op jit(solution)/shard_map/all_to_all | solution.py:15
  20.0 10.8 %all_gather.3 = bf16[768,256]{0,1:T(8,128)(2,1)S(1)} all-gather(bf16[768,64]{0,1:T(8,128)(2,1)S(1)} %copy-done), channel_id=1, replica_groups=mesh['x'=4,'c'=2,'z'=16,'y'=4] {'y'}, dimensions={1}, use_global_device_ids=true | all-gather | bytes 491520 | tf_op jit(solution)/shard_map/all_gather | solution.py:72
  30.8 37.7 %all-to-all-done = bf16[4,1024,512]{2,1,0:T(8,128)(2,1)} async-done(((bf16[4,1024,512]{2,1,0:T(8,128)(2,1)}), bf16[4,1024,512]{2,1,0:T(8,128)(2,1)}, u32[]{:S(2)}, u32[]{:S(2)}) %all-to-all-start) | async-done | bytes 4194336 | tf_op jit(solution)/shard_map/all_to_all | solution.py:15
  68.5 3.3 stack.4
  71.8 9.7 %all-to-all-start.1 = ((bf16[16,768,256]{1,2,0:T(8,128)(2,1)}), bf16[16,768,256]{1,2,0:T(8,128)(2,1)}, u32[]{:S(2)}, u32[]{:S(2)}) async-start(bf16[16,768,256]{1,2,0:T(8,128)(2,1)} %stack.4), calls=%async_computation.1 | async-start | bytes 12582912 | tf_op jit(solution)/shard_map/all_to_all | solution.py:75
  81.6 3.4 collective-permute-start.1
  85.1 268.2 %all-to-all-done.1 = bf16[16,768,256]{1,2,0:T(8,128)(2,1)} async-done(((bf16[16,768,256]{1,2,0:T(8,128)(2,1)}), bf16[16,768,256]{1,2,0:T(8,128)(2,1)}, u32[]{:S(2)}, u32[]{:S(2)}) %all-to-all-start.1) | async-done | bytes 6291488 | tf_op jit(solution)/shard_map/all_to_all | solution.py:75
  353.3 7.1 %fusion.28 = (f32[768]{0:T(1024)S(1)}, f32[512,768]{1,0:T(8,128)S(1)}) fusion(bf16[4096,512]{1,0:T(8,128)(2,1)} %bitcast, bf16[768,4096]{0,1:T(8,128)(2,1)} %bitcast.2), kind=kOutput, calls=%fused_computation.76 | convolution fusion | flops 3221617920 | bytes 12061696 | tf_op jit(solution)/shard_map/dot_general | solution.py:82
  360.4 7.1 %fusion.29 = (f32[768]{0:T(1024)S(1)}, f32[512,768]{1,0:T(8,128)S(1)}) fusion(bf16[4096,512]{1,0:T(8,128)(2,1)} %collective-permute-done.1, bf16[768,4096]{0,1:T(8,128)(2,1)} %bitcast.2), kind=kOutput, calls=%fused_computation.77 | convolution fusion | flops 3221617920 | bytes 12061696 | tf_op jit(solution)/shard_map/dot_general | solution.py:82
  367.6 0.8 fusion.4
  368.8 0.7 all_to_all.18
  369.5 14.6 %all-to-all-start.2 = ((f32[64,1,384]{2,1,0:T(1,128)}), f32[64,1,384]{2,1,0:T(1,128)S(1)}, u32[]{:S(2)}, u32[]{:S(2)}) async-start(f32[64,1,384]{2,1,0:T(1,128)} %all_to_all.18), calls=%async_computation.2 | async-start | bytes 196608 | tf_op jit(solution)/shard_map/all_to_all | solution.py:41
  384.6 14.3 %all-to-all-done.2 = f32[64,1,384]{2,1,0:T(1,128)S(1)} async-done(((f32[64,1,384]{2,1,0:T(1,128)}), f32[64,1,384]{2,1,0:T(1,128)S(1)}, u32[]{:S(2)}, u32[]{:S(2)}) %all-to-all-start.2) | async-done | bytes 98336 | tf_op jit(solution)/shard_map/all_to_all | solution.py:41
  398.9 0.2 reduce.5
  399.8 0.6 broadcast_in_dim.72
  400.4 6.2 %all-to-all-start.3 = ((f32[32,1,128]{2,1,0:T(1,128)}), f32[32,1,128]{2,1,0:T(1,128)S(1)}, u32[]{:S(2)}, u32[]{:S(2)}) async-start(f32[32,1,128]{2,1,0:T(1,128)} %broadcast_in_dim.72), calls=%async_computation.3 | async-start | bytes 32768 | tf_op jit(solution)/shard_map/all_to_all | solution.py:15
  406.7 0.5 fusion.25
  407.2 6.4 %all-to-all-done.3 = f32[32,1,128]{2,1,0:T(1,128)S(1)} async-done(((f32[32,1,128]{2,1,0:T(1,128)}), f32[32,1,128]{2,1,0:T(1,128)S(1)}, u32[]{:S(2)}, u32[]{:S(2)}) %all-to-all-start.3) | async-done | bytes 16416 | tf_op jit(solution)/shard_map/all_to_all | solution.py:15
  413.6 0.6 maximum_divide_fusion
  (36 shorter events, 1.5 us)
Async XLA Ops:
  1.9 10.3 %collective-permute-start = (bf16[512,512]{1,0:T(8,128)(2,1)S(1)}, bf16[512,512]{1,0:T(8,128)(2,1)S(1)}, u32[]{:S(2)}, u32[]{:S(2)}) collective-permute-start(bf16[512,512]{1,0:T(8,128)(2,1)S(1)} %get-tuple-element.17), channel_id=1, source_target_pairs={{0,64},{64,0},{1,65},{65,1},{2,66},{66,2},{3,67},{67,3},{4,68},{68... | collective-permute-start | bytes 1572872 | tf_op jit(solution)/shard_map/ppermute | solution.py:25
  14.9 5.1 %copy-start = (bf16[768,64]{0,1:T(8,128)(2,1)S(1)}, bf16[768,64]{0,1:T(8,128)(2,1)}, u32[]{:S(2)}) copy-start(bf16[768,64]{0,1:T(8,128)(2,1)} %param.5) | copy-start | bytes 294916
  14.9 53.6 %all-to-all-start = ((bf16[4,1024,512]{2,1,0:T(8,128)(2,1)}), bf16[4,1024,512]{2,1,0:T(8,128)(2,1)}, u32[]{:S(2)}, u32[]{:S(2)}) async-start(bf16[4,1024,512]{2,1,0:T(8,128)(2,1)} %broadcast_in_dim.65), calls=%async_computation | async-start | bytes 8388608 | tf_op jit(solution)/shard_map/all_to_all | solution.py:15
  71.8 13.2 %copy-start.3 = (s32[6]{0:T(128)S(1)}, s32[6]{0:T(128)}, u32[]{:S(2)}) copy-start(s32[6]{0:T(128)} %param.9) | copy-start | bytes 76
  71.8 281.5 %all-to-all-start.1 = ((bf16[16,768,256]{1,2,0:T(8,128)(2,1)}), bf16[16,768,256]{1,2,0:T(8,128)(2,1)}, u32[]{:S(2)}, u32[]{:S(2)}) async-start(bf16[16,768,256]{1,2,0:T(8,128)(2,1)} %stack.4), calls=%async_computation.1 | async-start | bytes 12582912 | tf_op jit(solution)/shard_map/all_to_all | solution.py:75
  81.6 278.9 %collective-permute-start.1 = (bf16[4096,512]{1,0:T(8,128)(2,1)}, bf16[4096,512]{1,0:T(8,128)(2,1)}, u32[]{:S(2)}, u32[]{:S(2)}) collective-permute-start(bf16[4096,512]{1,0:T(8,128)(2,1)} %bitcast), channel_id=1, source_target_pairs={{0,64},{64,0},{1,65},{65,1},{2,66},{66,2},{3,67},{67,3},{4,68},{68... | collective-permute-start | bytes 12582920 | tf_op jit(solution)/shard_map/ppermute | solution.py:31
  360.4 7.2 %copy-start.1 = (s32[768]{0:T(1024)S(1)}, s32[768]{0:T(1024)}, u32[]{:S(2)}) copy-start(s32[768]{0:T(1024)} %param.7) | copy-start | bytes 9220
  367.6 16.7 %copy-start.2 = (s32[768]{0:T(1024)S(1)}, s32[768]{0:T(1024)}, u32[]{:S(2)}) copy-start(s32[768]{0:T(1024)} %param.8) | copy-start | bytes 9220
  369.5 29.4 %all-to-all-start.2 = ((f32[64,1,384]{2,1,0:T(1,128)}), f32[64,1,384]{2,1,0:T(1,128)S(1)}, u32[]{:S(2)}, u32[]{:S(2)}) async-start(f32[64,1,384]{2,1,0:T(1,128)} %all_to_all.18), calls=%async_computation.2 | async-start | bytes 196608 | tf_op jit(solution)/shard_map/all_to_all | solution.py:41
  400.4 13.2 %all-to-all-start.3 = ((f32[32,1,128]{2,1,0:T(1,128)}), f32[32,1,128]{2,1,0:T(1,128)S(1)}, u32[]{:S(2)}, u32[]{:S(2)}) async-start(f32[32,1,128]{2,1,0:T(1,128)} %broadcast_in_dim.72), calls=%async_computation.3 | async-start | bytes 32768 | tf_op jit(solution)/shard_map/all_to_all | solution.py:15
